TPU v7x, 32 devices: a whole 2x2x4 slice. The times are simulated.
32 devices in a mesh: ctg: 8 (over y, x, core), br: 4 (over z).
Axes of the slice: x: 2, y: 2, z: 4, core: 2. Of those that a mesh axis runs over, the one named last changes fastest.
Arguments:
- base_vm: float32 [10240], P(('ctg', 'br')), may hold values from 0.95 to 1.05
- base_va: float32 [10240], P(('ctg', 'br')), may hold values from -0.6 to 0.6
- delta_state: float32 [64, 2, 10240], P('ctg', None, 'br'), may hold values from -0.18 to 0.18
- multipliers: float32 [64, 2, 10240], P('ctg', None, 'br'), may hold values from -6 to 6
- net_inj: float32 [64, 2, 10240], P('ctg', None, 'br'), may hold values from -6 to 6
- ang_grad: float32 [64, 10240], P('ctg', 'br'), may hold values from -6 to 6
- from_bus: int32 [13312], P('br'), may hold values from 0 to 10239
- to_bus: int32 [13312], P('br'), may hold values from 0 to 10239
- status: int32 [64, 13312], P('ctg', 'br'), may hold values 0 or 1
- conduct: float32 [13312], P('br'), may hold values from 1 to 5
- suscept: float32 [13312], P('br'), may hold values from -15 to -5
- charging: float32 [13312], P('br'), may hold values from 0.1 to 0.6
- rating: float32 [13312], P('br'), may hold values from 1 to 3
- slack: float32 [64, 13312], P('ctg', 'br'), may hold values from 0.05 to 2
- zdual: float32 [64, 13312], P('ctg', 'br'), may hold values from 0.05 to 2
Outputs:
- mismatch: float32 [64, 2, 10240], P('ctg', None, 'br')
- dual_res: float32 [64, 10240], P('ctg', 'br')
- limit_res: float32 [64, 13312], P('ctg', 'br')
- ctg_norms: float32 [64, 4], P('ctg')
- total_norms: float32 [4], replicated
All inputs are finite; a program needn't handle non-finite values. No bound on the sum of `status` on one device may be relied on, other than what follows from the above.
Results may differ from a plain program's by a relative error of at most 0.0003.
Values sent between devices are 32-bit elements; how exact they have to be, the bound alone decides.
A program may use at most 64 MiB of HBM per device.

v0:
```python
import functools

import jax
import jax.numpy as jnp
from jax import lax
from jax.experimental import pallas as pl
from jax.experimental.pallas import tpu as pltpu
from jax.sharding import PartitionSpec as P

LANES = 128
SPAN = 256
ROWS = 8
MESH = pl.DeviceIdType.MESH


def sin_cos(x):
    y = x * x
    sin_c = (1 / 6227020800, -1 / 39916800, 1 / 362880, -1 / 5040, 1 / 120, -1 / 6)
    cos_c = (-1 / 87178291200, 1 / 479001600, -1 / 3628800, 1 / 40320, -1 / 720, 1 / 24, -0.5)
    s = jnp.full_like(y, sin_c[0])
    for c in sin_c[1:]:
        s = s * y + c
    k = jnp.full_like(y, cos_c[0])
    for c in cos_c[1:]:
        k = k * y + c
    return x + x * y * s, 1.0 + y * k


def body(
    groups, ranks,
    base, delta, mult, net_any, ang_any, ends, params, rating, status3, status_any, slack_any, zdual_any,
    mis_out, dual_out, lim_out, norm_out, tot_out,
    bbuf, dbuf, mbuf, ebuf, pbuf, stbuf, table, acc,
    res, rbuf, flow, rflow, sqs, sqbuf, rowbuf,
    net, ang, status, slack, zdual, local,
    send, recv, base_send, base_recv, sq_send, sq_recv,
):
    grp, me = lax.axis_index("ctg"), lax.axis_index("br")
    count = groups * ranks
    mine = grp * ranks + me
    per = dbuf.shape[1]
    nb, nl = delta.shape[2], ends.shape[1]
    scen = delta.shape[0]

    own = pl.ds(me * per, per)
    local_copies = [
        pltpu.make_async_copy(a, b, local.at[i])
        for i, (a, b) in enumerate((
            (delta.at[own], dbuf.at[me]), (mult.at[own], mbuf.at[me]),
            (status_any, status), (slack_any, slack), (zdual_any, zdual),
            (net_any, net), (ang_any, ang),
        ))
    ]
    for copy in local_copies:
        copy.start()

    barrier = pltpu.get_barrier_semaphore()

    def greet(i, carry):
        peer = lax.rem(mine + i, count)
        pl.semaphore_signal(
            barrier, inc=1, device_id=(peer // ranks, lax.rem(peer, ranks)), device_id_type=MESH
        )
        return carry

    lax.fori_loop(1, count, greet, 0)
    pl.semaphore_wait(barrier, count - 1)

    def remote(src, dst, kind, step):
        return pltpu.make_async_remote_copy(
            src_ref=src, dst_ref=dst, send_sem=send.at[kind, step], recv_sem=recv.at[kind, step],
            device_id=(grp, lax.rem(me + step, ranks)), device_id_type=MESH,
        )

    def all_peers(slots, block, sends, recvs, i):
        peer = lax.rem(mine + i, count)
        return pltpu.make_async_remote_copy(
            src_ref=block, dst_ref=slots.at[mine], send_sem=sends.at[i], recv_sem=recvs.at[i],
            device_id=(peer // ranks, lax.rem(peer, ranks)), device_id_type=MESH,
        )

    def begin_base(i, c):
        all_peers(bbuf, base, base_send, base_recv, i).start()
        return c

    def finish_base(i, c):
        all_peers(bbuf, base, base_send, base_recv, i).wait()
        return c

    lax.fori_loop(1, count, begin_base, 0)
    first = []
    for step in range(1, ranks):
        peer = lax.rem(me + step, ranks)
        part = pl.ds(peer * per, per)
        first.append((
            remote(delta.at[part], dbuf.at[me], 0, step),
            remote(mult.at[part], mbuf.at[me], 1, step),
            remote(ends, ebuf.at[me], 2, step),
            remote(params, pbuf.at[me], 3, step),
            remote(status3.at[peer], stbuf.at[me], 4, step),
        ))
    for kind in range(5):
        for group in first:
            group[kind].start()

    bbuf[mine] = base[...]
    ebuf[me] = ends[...]
    pbuf[me] = params[...]
    stbuf[me] = status3[me]
    table[...] = jnp.zeros_like(table)
    acc[...] = jnp.zeros_like(acc)
    sqs[...] = jnp.zeros_like(sqs)
    for copy in local_copies:
        copy.wait()
    live_own = status[...].astype(jnp.float32)
    comp = live_own * (zdual[...] * slack[...] - 0.01)
    sqs[:, 3:4] = jnp.sum(comp * comp, axis=1, keepdims=True)

    lax.fori_loop(1, count, finish_base, 0)
    for group in first:
        for copy in group[:3]:
            copy.wait()

    for src in range(ranks):
        cols = slice(src * nb, (src + 1) * nb)
        volts = jnp.concatenate([bbuf[src * groups + i] for i in range(groups)], axis=1)
        for s in range(per):
            table[s : s + 1, cols] = volts[0:1] + dbuf[src, s, 0:1, :]
            table[per + s : per + s + 1, cols] = volts[1:2] + dbuf[src, s, 1:2, :]
            table[2 * per + s : 2 * per + s + 1, cols] = mbuf[src, s, 0:1, :]
            table[3 * per + s : 3 * per + s + 1, cols] = mbuf[src, s, 1:2, :]

    tiles = table.shape[1] // LANES
    high = table.shape[1] // SPAN

    chunk = SPAN if nl % SPAN == 0 else LANES
    pieces = nl // chunk
    bf16 = jnp.bfloat16

    def place(i):
        return lax.rem(me - i // pieces + ranks, ranks), pl.ds(pl.multiple_of(lax.rem(i, pieces) * chunk, chunk), chunk)

    def pick(i):
        src, cols = place(i)
        picked = []
        for end in range(2):
            spots = jnp.broadcast_to(ebuf[src, end : end + 1, cols], (ROWS, chunk))
            tiles_found = []
            for at in range(0, chunk, LANES):
                spot = spots[:, at : at + LANES]
                low, tile = spot & (LANES - 1), spot >> 7
                found = jnp.zeros((ROWS, LANES), jnp.float32)
                for k in range(tiles):
                    piece = jnp.take_along_axis(
                        table[:, k * LANES : (k + 1) * LANES], low, axis=1, mode="promise_in_bounds"
                    )
                    found = jnp.where(tile == k, piece, found)
                tiles_found.append(found)
            picked.append(jnp.concatenate(tiles_found, axis=1))
        return tuple(picked)

    def process(i, picked):
        src, cols = place(i)

        def quantity(end, q):
            return picked[end][q * per : (q + 1) * per, :]

        vf, vt = quantity(0, 0), quantity(1, 0)
        sn, cs = sin_cos(quantity(0, 1) - quantity(1, 1))
        par = pbuf[src, :, cols]
        g, b, h = par[0:1], par[1:2], par[2:3]
        live = stbuf[src, :, cols].astype(jnp.float32)
        u = vf * vt
        gc_bs, gc_mbs = g * cs + b * sn, g * cs - b * sn
        gs_bc, gs_mbc = g * sn + b * cs, g * sn - b * cs
        bh = -(b + h)
        pf = live * (g * vf * vf - u * gc_bs)
        qf = live * (bh * vf * vf - u * gs_mbc)
        pt = live * (g * vt * vt - u * gc_mbs)
        qt = live * (bh * vt * vt + u * gs_bc)
        fd = live * u * (
            quantity(0, 2) * gs_mbc - quantity(0, 3) * gc_bs
            + quantity(1, 2) * gs_bc + quantity(1, 3) * gc_mbs
        )
        flow[src, :, cols] = pf * pf + qf * qf
        blank = [jnp.zeros((ROWS - 3 * per, chunk), jnp.float32)]
        lefts, hots = [], []
        label = lax.broadcasted_iota(jnp.int32, (SPAN, chunk), 0).astype(bf16)
        for end, terms in ((0, [pf, qf, fd]), (1, [pt, qt, -fd])):
            value = jnp.concatenate(terms + blank, axis=0)
            head = value.astype(bf16).astype(jnp.float32)
            both = jnp.concatenate([head, value - head], axis=0).astype(bf16)
            spot = ebuf[src, end : end + 1, cols]
            row = jnp.broadcast_to(spot >> 8, (2 * ROWS, chunk)).astype(bf16)
            low = jnp.broadcast_to((spot & (SPAN - 1)), (2 * ROWS, chunk)).astype(bf16)
            low = jnp.concatenate([low] * (SPAN // (2 * ROWS)), axis=0)
            hots.append(jnp.where(low == label, bf16(1), bf16(0)))
            lefts.append(jnp.concatenate(
                [jnp.where(row == bf16(k), both, bf16(0)) for k in range(high)], axis=0
            ))
        acc[...] += lax.dot_general(
            jnp.concatenate(lefts, axis=1), jnp.concatenate(hots, axis=1),
            (((1,), (1,)), ((), ())), preferred_element_type=jnp.float32,
        )

    final = ranks * pieces - 1

    def one_step(step, picked):
        src = lax.rem(me - step + ranks, ranks)

        @pl.when(step > 0)
        def _():
            remote(params, pbuf.at[me], 3, step).wait()
            remote(status3.at[0], stbuf.at[me], 4, step).wait()

        def advance(t, picked):
            i = step * pieces + t
            following = pick(jnp.minimum(i + 1, final))
            process(i, picked)
            return following

        picked = lax.fori_loop(0, pieces, advance, picked)

        @pl.when(step > 0)
        def _():
            remote(flow.at[src], rflow.at[me], 6, ranks - step).start()

        return picked

    lax.fori_loop(0, ranks, one_step, pick(0))

    for k in range(high):
        at = k * SPAN
        row = k * 2 * ROWS
        sums = acc[row : row + ROWS, :] + acc[row + ROWS : row + 2 * ROWS, :]
        for q in range(3):
            res[at // nb, q, :, at % nb : at % nb + SPAN] = sums[q * per : (q + 1) * per, :]

    back = []
    for step in range(1, ranks):
        peer = lax.rem(me + step, ranks)
        back.append((
            remote(res.at[peer], rbuf.at[me], 5, step),
        ))
    for group in back:
        group[0].start()
    rbuf[me] = res[me]
    rflow[me] = flow[me]
    for step in range(1, ranks):
        remote(flow.at[me], rflow.at[me], 6, step).wait()
    for group in back:
        group[0].wait()

    rate = rating[...] * rating[...]
    for src in range(ranks):
        for s in range(per):
            c = src * per + s
            total = jnp.zeros((1, 1), jnp.float32)
            for k in range(2):
                row = rbuf[src, k, s : s + 1, :] - net[c, k : k + 1, :]
                mis_out[c, k : k + 1, :] = row
                total = total + jnp.sum(row * row, axis=1, keepdims=True)
            sqs[c : c + 1, 0:1] = total
        rows = slice(src * per, (src + 1) * per)
        dual = rbuf[src, 2] + ang[rows, :]
        dual_out[rows, :] = dual
        sqs[rows, 1:2] = jnp.sum(dual * dual, axis=1, keepdims=True)
        lim = status[rows, :].astype(jnp.float32) * (rflow[src] + slack[rows, :] - rate)
        lim_out[rows, :] = lim
        sqs[rows, 2:3] = jnp.sum(lim * lim, axis=1, keepdims=True)

    sqbuf[me] = sqs[...]
    rowbuf[mine] = jnp.sum(sqs[...], axis=0, keepdims=True)
    near = [remote(sqbuf.at[me], sqbuf.at[me], 7, step) for step in range(1, ranks)]
    for copy in near:
        copy.start()

    def begin(i, c):
        all_peers(rowbuf, rowbuf.at[mine], sq_send, sq_recv, i).start()
        return c

    def finish(i, c):
        all_peers(rowbuf, rowbuf.at[mine], sq_send, sq_recv, i).wait()
        return c

    lax.fori_loop(1, count, begin, 0)
    for copy in near:
        copy.wait()
    lax.fori_loop(1, count, finish, 0)

    def add(i, c):
        return c + rowbuf[i]

    zero = jnp.zeros((scen, LANES), jnp.float32)
    group_sum = zero
    for z in range(ranks):
        group_sum = group_sum + sqbuf[z]
    norm_out[...] = jnp.sqrt(group_sum[:, 0:4])
    everything = lax.fori_loop(0, count, add, jnp.zeros((1, LANES), jnp.float32))
    tot_out[...] = jnp.sqrt(everything[:, 0:4] / (scen * groups))


def per_device(
    base_vm, base_va, delta_state, multipliers, net_inj, ang_grad, from_bus, to_bus,
    status, conduct, suscept, charging, rating, slack, zdual,
):
    groups, ranks = lax.axis_size("ctg"), lax.axis_size("br")
    count = groups * ranks
    scen, _, nb = delta_state.shape
    nl = from_bus.shape[0]
    per = scen // ranks
    buses = nb * ranks
    high = buses // SPAN
    base = jnp.stack([base_vm, base_va])
    ends = jnp.stack([from_bus, to_bus])
    params = jnp.stack([conduct, suscept, charging])
    f32 = jnp.float32
    vmem = pl.BlockSpec(memory_space=pltpu.VMEM)
    hbm = pl.BlockSpec(memory_space=pl.ANY)
    mis, dual, lim, norms, tot = pl.pallas_call(
        functools.partial(body, groups, ranks),
        out_shape=(
            jax.ShapeDtypeStruct((scen, 2, nb), f32),
            jax.ShapeDtypeStruct((scen, nb), f32),
            jax.ShapeDtypeStruct((scen, nl), f32),
            jax.ShapeDtypeStruct((scen, 4), f32),
            jax.ShapeDtypeStruct((1, 4), f32),
        ),
        in_specs=[vmem, hbm, hbm, hbm, hbm, vmem, vmem, vmem, vmem, hbm, hbm, hbm],
        out_specs=(vmem,) * 5,
        scratch_shapes=[
            pltpu.VMEM((count, 2, base_vm.shape[0]), f32),
            pltpu.VMEM((ranks, per, 2, nb), f32),
            pltpu.VMEM((ranks, per, 2, nb), f32),
            pltpu.VMEM((ranks, 2, nl), jnp.int32),
            pltpu.VMEM((ranks, 3, nl), f32),
            pltpu.VMEM((ranks, per, nl), jnp.int32),
            pltpu.VMEM((ROWS, buses), f32),
            pltpu.VMEM((high * 2 * ROWS, SPAN), f32),
            pltpu.VMEM((ranks, 3, per, nb), f32),
            pltpu.VMEM((ranks, 3, per, nb), f32),
            pltpu.VMEM((ranks, per, nl), f32),
            pltpu.VMEM((ranks, per, nl), f32),
            pltpu.VMEM((scen, LANES), f32),
            pltpu.VMEM((ranks, scen, LANES), f32),
            pltpu.VMEM((count, 1, LANES), f32),
            pltpu.VMEM((scen, 2, nb), f32),
            pltpu.VMEM((scen, nb), f32),
            pltpu.VMEM((scen, nl), jnp.int32),
            pltpu.VMEM((scen, nl), f32),
            pltpu.VMEM((scen, nl), f32),
            pltpu.SemaphoreType.DMA((7,)),
            pltpu.SemaphoreType.DMA((8, ranks)),
            pltpu.SemaphoreType.DMA((8, ranks)),
            pltpu.SemaphoreType.DMA((count,)),
            pltpu.SemaphoreType.DMA((count,)),
            pltpu.SemaphoreType.DMA((count,)),
            pltpu.SemaphoreType.DMA((count,)),
        ],
        compiler_params=pltpu.CompilerParams(
            collective_id=0, has_side_effects=True, vmem_limit_bytes=48 << 20
        ),
    )(
        base, delta_state, multipliers, net_inj, ang_grad, ends, params, rating[None, :],
        status.reshape(ranks, per, nl), status, slack, zdual,
    )
    return (mis, dual, lim, norms, tot[0])


def solution(mesh):
    placed = (
        P(("ctg", "br")), P(("ctg", "br")),
        P("ctg", None, "br"), P("ctg", None, "br"), P("ctg", None, "br"), P("ctg", "br"),
        P("br"), P("br"), P("ctg", "br"), P("br"), P("br"), P("br"), P("br"),
        P("ctg", "br"), P("ctg", "br"),
    )
    return jax.shard_map(
        per_device,
        mesh=mesh,
        in_specs=placed,
        out_specs=(P("ctg", None, "br"), P("ctg", "br"), P("ctg", "br"), P("ctg", None), P()),
        check_vma=False,
    )
```

profile of v0, /device:TPU:0, one launch (start us, length us, event | category | flops | bytes accessed | tf_op | source)
XLA Modules:
  0.0 73.9 jit_solution(6968746084996776235)
XLA Ops:
  0.6 0.0 copy-start.11
  0.6 0.0 copy-start.10
  0.7 0.7 stack.30
  1.3 0.0 copy-done.11
  1.4 0.0 copy-start.7
  1.4 0.0 copy-start.8
  1.4 0.0 copy-start.9
  1.4 0.7 stack.33
  2.1 0.0 copy-done.7
  2.1 0.0 copy-start.2
  2.2 0.0 copy-done.8
  2.2 0.0 copy-start
  2.3 0.0 copy-done.9
  2.3 0.0 copy-done.10
  2.3 0.0 copy-start.1
  2.4 0.8 %broadcast_in_dim.3.rating = f32[1,3328]{1,0:T(1,128)S(1)} reshape(f32[3328]{0:T(1024)} %param.27) | data formatting | bytes 26624 | tf_op jit(solution)/shard_map/broadcast_in_dim | solution.py:364
  3.1 0.0 copy-done
  3.2 0.1 reshape.13.status3
  3.2 0.0 copy-done.2
  3.2 0.0 copy-done.1
  3.3 0.0 copy-start.3
  3.3 0.9 %copy-done.3 = f32[8,2,2560]{2,1,0:T(2,128)S(1)} copy-done((f32[8,2,2560]{2,1,0:T(2,128)S(1)}, f32[8,2,2560]{2,1,0:T(2,128)}, u32[]{:S(2)}) %copy-start.3) | copy-done | bytes 163864
  4.2 0.0 copy-start.4
  4.2 0.9 %copy-done.4 = f32[8,3328]{1,0:T(8,128)S(1)} copy-done((f32[8,3328]{1,0:T(8,128)S(1)}, f32[8,3328]{1,0:T(8,128)}, u32[]{:S(2)}) %copy-start.4) | copy-done | bytes 106520
  5.1 0.0 copy-start.5
  5.1 0.9 %copy-done.5 = f32[8,3328]{1,0:T(8,128)S(1)} copy-done((f32[8,3328]{1,0:T(8,128)S(1)}, f32[8,3328]{1,0:T(8,128)}, u32[]{:S(2)}) %copy-start.5) | copy-done | bytes 106520
  6.0 0.0 copy-start.6
  6.0 0.9 %copy-done.6 = f32[8,2560]{1,0:T(8,128)S(1)} copy-done((f32[8,2560]{1,0:T(8,128)S(1)}, f32[8,2560]{1,0:T(8,128)}, u32[]{:S(2)}) %copy-start.6) | copy-done | bytes 81944
  6.8 64.0 %shard_map.182 = (f32[8,2,2560]{2,1,0:T(2,128)S(1)}, f32[8,2560]{1,0:T(8,128)S(1)}, f32[8,3328]{1,0:T(8,128)S(1)}, f32[8,4]{1,0:T(8,128)S(1)}, f32[1,4]{1,0:T(1,128)S(1)}) custom-call(f32[2,320]{1,0:T(2,128)S(1)} %pad_maximum_fusion.1.base, f32[8,2,2560]{2,1,0:T(2,128)S(1)} %copy-done.1, f32[8,2,2560]{2,1,0:T(2,128)S(1)} %copy-done.2, ...), custom_call_target="tpu_custom_call" | custom-call | tf_op jit(solution)/shard_map/pallas_call | solution.py:320
  70.8 0.7 copy.20
  71.5 0.7 copy.25
  72.1 0.6 copy.26
  72.8 0.6 copy.27
  73.4 0.5 copy.28
  (8 shorter events, 0.1 us)
Async XLA Ops:
  0.6 0.7 copy-start.11
  0.6 1.6 %copy-start.10 = (f32[3328]{0:T(1024)S(1)}, f32[3328]{0:T(1024)}, u32[]{:S(2)}) copy-start(f32[3328]{0:T(1024)} %param.26) | copy-start | bytes 39940
  1.4 0.8 %copy-start.7 = (s32[3328]{0:T(1024)S(1)}, s32[3328]{0:T(1024)}, u32[]{:S(2)}) copy-start(s32[3328]{0:T(1024)} %param.22) | copy-start | bytes 39940
  1.4 0.8 %copy-start.8 = (f32[3328]{0:T(1024)S(1)}, f32[3328]{0:T(1024)}, u32[]{:S(2)}) copy-start(f32[3328]{0:T(1024)} %param.24) | copy-start | bytes 39940
  1.4 0.9 %copy-start.9 = (f32[3328]{0:T(1024)S(1)}, f32[3328]{0:T(1024)}, u32[]{:S(2)}) copy-start(f32[3328]{0:T(1024)} %param.25) | copy-start | bytes 39940
  2.1 1.1 %copy-start.2 = (f32[8,2,2560]{2,1,0:T(2,128)S(1)}, f32[8,2,2560]{2,1,0:T(2,128)}, u32[]{:S(2)}) copy-start(f32[8,2,2560]{2,1,0:T(2,128)} %mult.1) | copy-start | bytes 491524
  2.2 0.9 %copy-start = (s32[8,3328]{1,0:T(8,128)S(1)}, s32[8,3328]{1,0:T(8,128)}, u32[]{:S(2)}) copy-start(s32[8,3328]{1,0:T(8,128)} %status_any.1) | copy-start | bytes 319492
  2.3 0.9 %copy-start.1 = (f32[8,2,2560]{2,1,0:T(2,128)S(1)}, f32[8,2,2560]{2,1,0:T(2,128)}, u32[]{:S(2)}) copy-start(f32[8,2,2560]{2,1,0:T(2,128)} %delta.1) | copy-start | bytes 491524
  3.3 0.9 %copy-start.3 = (f32[8,2,2560]{2,1,0:T(2,128)S(1)}, f32[8,2,2560]{2,1,0:T(2,128)}, u32[]{:S(2)}) copy-start(f32[8,2,2560]{2,1,0:T(2,128)} %net_any.1) | copy-start | bytes 491524
  4.2 0.9 %copy-start.4 = (f32[8,3328]{1,0:T(8,128)S(1)}, f32[8,3328]{1,0:T(8,128)}, u32[]{:S(2)}) copy-start(f32[8,3328]{1,0:T(8,128)} %slack_any.1) | copy-start | bytes 319492
  5.1 0.9 %copy-start.5 = (f32[8,3328]{1,0:T(8,128)S(1)}, f32[8,3328]{1,0:T(8,128)}, u32[]{:S(2)}) copy-start(f32[8,3328]{1,0:T(8,128)} %zdual_any.1) | copy-start | bytes 319492
  6.0 0.9 %copy-start.6 = (f32[8,2560]{1,0:T(8,128)S(1)}, f32[8,2560]{1,0:T(8,128)}, u32[]{:S(2)}) copy-start(f32[8,2560]{1,0:T(8,128)} %ang_any.1) | copy-start | bytes 245764
where the time goes:
time: 74.3 us; the launch traced here: 73.9 us
  Pallas kernels  64 us (86%)
  local copies, waits for them, and re-layouts  9.08 us (12%)
  between operations  0.81 us (1%)
    pallas_call x1, Pallas kernels, per_device(): pl.pallas_call(functools.partial(body, groups, ranks), out_shape=(jax.Sha...  64 us
    unnamed x29, local copies, waits for them, and re-layouts  6.77 us

commit v1 on v0

v1 whole, which is shorter than its diff:
```python
import functools
import math

import jax
import jax.numpy as jnp
from jax import lax
from jax.experimental import pallas as pl
from jax.experimental.pallas import tpu as pltpu
from jax.sharding import PartitionSpec as P

LANES = 128
SPAN = 256
SUB = 8
PACK = 16
MESH = pl.DeviceIdType.MESH


def sin_cos(x):
    y = x * x
    sin_c = (1 / 6227020800, -1 / 39916800, 1 / 362880, -1 / 5040, 1 / 120, -1 / 6)
    cos_c = (-1 / 87178291200, 1 / 479001600, -1 / 3628800, 1 / 40320, -1 / 720, 1 / 24, -0.5)
    s = jnp.full_like(y, sin_c[0])
    for c in sin_c[1:]:
        s = s * y + c
    k = jnp.full_like(y, cos_c[0])
    for c in cos_c[1:]:
        k = k * y + c
    return x + x * y * s, 1.0 + y * k


def packing(per):
    width = 6 * per
    group = width * PACK // math.gcd(width, PACK)
    starts = [(SUB * h) % width for h in range(group // SUB)]
    return width, group, starts, max(starts) + SUB


def body(
    groups, ranks,
    bvm, bva, delta, mult, net_h, ang_h, frm, to, status_t, con, sus, cha, rat, status_h, slack_h, zdual_h,
    mis_out, dual_out, lim_out, norm_out, tot_out,
    bown, bslot, volts, table, ends, par, stat, picks, vals, acc, res, rbuf, flow, rflow,
    sqs, sqbuf, rowbuf, net, ang, status, slack, zdual, rate,
    local, send, recv, base_send, base_recv, sq_send, sq_recv,
):
    grp, me = lax.axis_index("ctg"), lax.axis_index("br")
    count = groups * ranks
    mine = grp * ranks + me
    scen, _, nb = delta.shape
    per = scen // ranks
    rows = frm.shape[0]
    total = rows * ranks
    pad = rflow.shape[0] // scen
    bf16 = jnp.bfloat16

    def cols_of(src):
        return pl.ds(pl.multiple_of(src * nb, LANES), nb)

    def rows_of(src):
        return pl.ds(src * rows, rows)

    def scen_of(src):
        return pl.ds(src * per, per)

    pairs = [(bvm, bown.at[0, 0]), (bva, bown.at[1, 0])]
    pairs += [(delta.at[:, q], volts.at[q]) for q in range(2)]
    pairs += [(frm, ends.at[0, rows_of(me)]), (to, ends.at[1, rows_of(me)])]
    pairs += [(p, par.at[i, rows_of(me)]) for i, p in enumerate((con, sus, cha))]
    early = len(pairs)
    pairs += [(delta.at[scen_of(me), q], table.at[pl.ds(q * per, per), cols_of(me)]) for q in range(2)]
    pairs += [(mult.at[scen_of(me), q], table.at[pl.ds((2 + q) * per, per), cols_of(me)]) for q in range(2)]
    pairs += [(status_t.at[:, me * per + s], stat.at[s, rows_of(me)]) for s in range(per)]
    middle = len(pairs)
    pairs += [(net_h.at[:, q], net.at[q]) for q in range(2)]
    pairs += [(ang_h, ang), (status_h, status), (slack_h, slack), (zdual_h, zdual), (rat, rate)]
    copies = [pltpu.make_async_copy(a, b, local.at[i]) for i, (a, b) in enumerate(pairs)]
    for copy in copies:
        copy.start()

    barrier = pltpu.get_barrier_semaphore()

    def greet(i, carry):
        peer = lax.rem(mine + i, count)
        pl.semaphore_signal(
            barrier, inc=1, device_id=(peer // ranks, lax.rem(peer, ranks)), device_id_type=MESH
        )
        return carry

    lax.fori_loop(1, count, greet, 0)
    acc[...] = jnp.zeros_like(acc)
    sqs[...] = jnp.zeros_like(sqs)
    for copy in copies[:early]:
        copy.wait()
    pl.semaphore_wait(barrier, count - 1)

    def toward(step):
        return lax.rem(me - step + ranks, ranks)

    def origin(step):
        return lax.rem(me + step, ranks)

    def remote(src, dst, kind, step):
        return pltpu.make_async_remote_copy(
            src_ref=src, dst_ref=dst, send_sem=send.at[kind, step], recv_sem=recv.at[kind, step],
            device_id=(grp, toward(step)), device_id_type=MESH,
        )

    def send_ends(step):
        return [remote(ends.at[:, rows_of(me)], ends.at[:, rows_of(me)], 0, step)]

    def send_mult(step):
        return [
            remote(mult.at[scen_of(toward(step)), q], table.at[pl.ds((2 + q) * per, per), cols_of(me)], 1 + q, step)
            for q in range(2)
        ]

    def send_volts(step):
        return [
            remote(volts.at[q, scen_of(toward(step))], table.at[pl.ds(q * per, per), cols_of(me)], 3 + q, step)
            for q in range(2)
        ]

    def send_par(step):
        return [remote(par.at[:, rows_of(me)], par.at[:, rows_of(me)], 5, step)] + [
            remote(status_t.at[:, toward(step) * per + s], stat.at[s, rows_of(me)], 6 + s, step)
            for s in range(per)
        ]

    def send_res(step):
        return [remote(res.at[toward(step)], rbuf.at[:, scen_of(me)], 6 + per, step)]

    def send_flow(step):
        return [
            remote(flow.at[s, rows_of(toward(step))], rflow.at[pl.ds((me * per + s) * pad, rows)], 7 + per + s, step)
            for s in range(per)
        ]

    def send_sq(step):
        return [remote(sqbuf.at[me], sqbuf.at[me], 7 + 2 * per, step)]

    for step in range(1, ranks):
        for copy in send_ends(step):
            copy.start()

    home = mine // groups

    def base_copy(i):
        return pltpu.make_async_remote_copy(
            src_ref=bown, dst_ref=bslot.at[mine - home * groups],
            send_sem=base_send.at[i], recv_sem=base_recv.at[mine - home * groups],
            device_id=(i, home), device_id_type=MESH,
        )

    def begin_base(i, c):
        @pl.when(jnp.logical_or(i != grp, home != me))
        def _():
            base_copy(i).start()
        return c

    lax.fori_loop(0, groups, begin_base, 0)

    @pl.when(home == me)
    def _():
        bslot[mine - me * groups] = bown[...]

    for step in range(1, ranks):
        for copy in send_mult(step):
            copy.start()

    def end_base(i, c):
        @pl.when(jnp.logical_or(i != grp, home != me))
        def _():
            base_copy(i).wait_send()

        @pl.when(me * groups + i != mine)
        def _():
            pltpu.make_async_remote_copy(
                src_ref=bown, dst_ref=bslot.at[i], send_sem=base_send.at[i], recv_sem=base_recv.at[i],
                device_id=(i, home), device_id_type=MESH,
            ).wait_recv()
        return c

    lax.fori_loop(0, groups, end_base, 0)
    for copy in copies[early:middle]:
        copy.wait()
    for q in range(2):
        base = jnp.concatenate([bslot[i, q] for i in range(groups)], axis=1)
        volts[q] = volts[q] + base
        table[q * per : (q + 1) * per, cols_of(me)] = table[q * per : (q + 1) * per, cols_of(me)] + base

    for step in range(1, ranks):
        for copy in send_volts(step):
            copy.start()
    for step in range(1, ranks):
        for copy in send_par(step):
            copy.start()

    tiles = nb // LANES

    def look(spot, src, found):
        low, tile = spot & (LANES - 1), (spot >> 7) - src * tiles
        for k in range(tiles):
            piece = jnp.take_along_axis(
                table[:, pl.ds(pl.multiple_of(src * nb + k * LANES, LANES), LANES)],
                low, axis=1, mode="promise_in_bounds",
            )
            found = jnp.where(tile == k, piece, found)
        return found

    def spot_of(end, r):
        return jnp.broadcast_to(ends[end, pl.ds(r, 1), :], (SUB, LANES))

    def slot_of(r):
        return pl.ds(pl.multiple_of(r * SUB, SUB), SUB)

    unroll = 2 if rows % 2 == 0 else 1
    early_steps = max(1, ranks // 2)

    def scan_rows(src, block, fresh):
        def some(t, c):
            for o in range(unroll):
                r = block * rows + t * unroll + o
                for end in range(2):
                    start = jnp.zeros((SUB, LANES), jnp.float32) if fresh else picks[end, slot_of(r), :]
                    picks[end, slot_of(r), :] = look(spot_of(end, r), src, start)
            return c

        lax.fori_loop(0, rows // unroll, some, 0)

    for block in range(ranks):
        if block > 0:
            for copy in send_ends(block):
                copy.wait()
        scan_rows(me, origin(block), True)
    for step in range(1, early_steps):
        for copy in send_mult(step) + send_volts(step):
            copy.wait()
        lax.fori_loop(0, ranks, lambda b, c, step=step: (scan_rows(origin(step), b, False), c)[1], 0)
    for step in range(early_steps, ranks):
        for copy in send_mult(step) + send_volts(step):
            copy.wait()

    for copy in copies[middle:]:
        copy.wait()

    chunks = total // SUB
    first = (me * rows + SUB - 1) // SUB
    ahead = first * SUB - me * rows

    def chunk_of(i):
        return lax.rem(first + i, chunks)

    def pick(i):
        at = chunk_of(i) * SUB
        for end in range(2):
            for t in range(SUB):
                r = at + t
                spot = spot_of(end, r)
                found = picks[end, slot_of(r), :]
                for step in range(early_steps, ranks):
                    found = look(spot, origin(step), found)
                picks[end, slot_of(r), :] = found

    width, group, starts, entries = packing(per)
    spans = table.shape[1] // SPAN
    tps = group // width
    parts = group // PACK
    iota16 = lax.broadcasted_iota(jnp.int32, (PACK, LANES), 0)
    label = lax.broadcasted_iota(jnp.int32, (SPAN, LANES), 0).astype(bf16)
    shift = [((iota16 + PACK * p) // width).astype(bf16) for p in range(parts)]

    def process(i):
        at = pl.multiple_of(chunk_of(i) * SUB, SUB)
        here = pl.ds(at, SUB)

        def quantity(end, q, s):
            return picks[end, pl.ds(at * SUB + q * per + s, SUB, stride=SUB), :]

        seen = [[[quantity(end, q, s) for s in range(per)] for q in range(4)] for end in range(2)]
        pick(jnp.minimum(i + 1, chunks - 1))
        g, b, h = par[0, here, :], par[1, here, :], par[2, here, :]
        bh = -(b + h)
        for s in range(per):
            live = stat[s, here, :].astype(jnp.float32)
            vf, vt = seen[0][0][s], seen[1][0][s]
            sn, cs = sin_cos(seen[0][1][s] - seen[1][1][s])
            u = vf * vt
            gc_bs, gc_mbs = g * cs + b * sn, g * cs - b * sn
            gs_bc, gs_mbc = g * sn + b * cs, g * sn - b * cs
            pf = live * (g * vf * vf - u * gc_bs)
            qf = live * (bh * vf * vf - u * gs_mbc)
            pt = live * (g * vt * vt - u * gc_mbs)
            qt = live * (bh * vt * vt + u * gs_bc)
            fd = live * u * (
                seen[0][2][s] * gs_mbc - seen[0][3][s] * gc_bs
                + seen[1][2][s] * gs_bc + seen[1][3][s] * gc_mbs
            )
            flow[s, here, :] = pf * pf + qf * qf
            for end, terms in ((0, (pf, qf, fd)), (1, (pt, qt, -fd))):
                for q, term in enumerate(terms):
                    head = term.astype(bf16).astype(jnp.float32)
                    tail = term - head
                    for v, x in ((q * per + s, head), ((3 + q) * per + s, tail)):
                        for e in range(v, entries, width):
                            vals[end, e * SUB : (e + 1) * SUB, :] = x
        sums = None
        for end in range(2):
            for pair in range(SUB // 2):
                lefts, hots = [], []
                for t in (2 * pair, 2 * pair + 1):
                    spot = jnp.broadcast_to(ends[end, pl.ds(at + t, 1), :], (PACK, LANES))
                    high = (spot >> 8).astype(bf16)
                    low = (spot & (SPAN - 1)).astype(bf16)
                    low = jnp.concatenate([low] * (SPAN // PACK), axis=0)
                    hots.append(jnp.where(low == label, bf16(1), bf16(0)))
                    half = {
                        s0: vals[end, pl.ds(s0 * SUB + t, SUB, stride=SUB), :] for s0 in set(starts)
                    }
                    tile = [
                        jnp.concatenate([half[starts[2 * p]], half[starts[2 * p + 1]]], axis=0).astype(bf16)
                        for p in range(parts)
                    ]
                    level = [high - shift[p] for p in range(parts)]
                    lefts.append(jnp.concatenate([
                        jnp.where(level[p] == bf16(j * tps), tile[p], bf16(0))
                        for j in range(spans // tps) for p in range(parts)
                    ], axis=0))
                term = lax.dot_general(
                    jnp.concatenate(lefts, axis=1), jnp.concatenate(hots, axis=1),
                    (((1,), (1,)), ((), ())), preferred_element_type=jnp.float32,
                )
                sums = term if sums is None else sums + term
        acc[...] += sums

    pick(0)

    def advance(i, c):
        done = ahead + i * SUB

        for step in range(1, ranks):
            @pl.when(jnp.logical_and(done + SUB > step * rows, jnp.logical_or(done <= step * rows, i == 0)))
            def _(step=step):
                for copy in send_par(step):
                    copy.wait()

        process(i)

        for step in range(1, ranks):
            @pl.when(jnp.logical_and(done + SUB >= (step + 1) * rows, done < (step + 1) * rows))
            def _(step=step):
                for copy in send_flow(ranks - step):
                    copy.start()
        return c

    lax.fori_loop(0, chunks, advance, 0)

    quarter = nb // SPAN
    for dest in range(ranks):
        for k in range(dest * quarter, (dest + 1) * quarter):
            row = (k // tps) * group + (k % tps) * width
            both = acc[row : row + 3 * per, :] + acc[row + 3 * per : row + width, :]
            for q in range(3):
                at = (k - dest * quarter) * SPAN
                res[dest, q, :, at : at + SPAN] = both[q * per : (q + 1) * per, :]

        @pl.when(dest == me)
        def _(dest=dest):
            for q in range(3):
                rbuf[q, dest * per : (dest + 1) * per, :] = res[dest, q]

        for step in range(1, ranks):
            @pl.when(dest == toward(step))
            def _(step=step):
                for copy in send_res(step):
                    copy.start()

    for dest in range(ranks):
        @pl.when(dest == me)
        def _(dest=dest):
            for s in range(per):
                at = (dest * per + s) * pad
                rflow[at : at + rows, :] = flow[s, dest * rows : (dest + 1) * rows, :]

    live_own = status[...].astype(jnp.float32)
    comp = live_own * (zdual[...] * slack[...] - 0.01)
    sqs[:, 3:4] = jnp.sum(comp * comp, axis=1, keepdims=True)
    for step in range(1, ranks):
        for copy in send_flow(step):
            copy.wait()
    power = jnp.zeros((scen, LANES), jnp.float32)
    for r in range(rows):
        at = slice(r * LANES, (r + 1) * LANES)
        limit = rate[r : r + 1, :]
        lim = status[:, at].astype(jnp.float32) * (
            rflow[pl.ds(r, scen, stride=pad), :] + slack[:, at] - limit * limit
        )
        lim_out[:, at] = lim
        power = power + lim * lim
    sqs[:, 2:3] = jnp.sum(power, axis=1, keepdims=True)

    for step in range(1, ranks):
        for copy in send_res(step):
            copy.wait()
    power = None
    for q in range(2):
        row = rbuf[q] - net[q]
        mis_out[q] = row
        power = row * row if power is None else power + row * row
    sqs[:, 0:1] = jnp.sum(power, axis=1, keepdims=True)
    dual = rbuf[2] + ang[...]
    dual_out[...] = dual
    sqs[:, 1:2] = jnp.sum(dual * dual, axis=1, keepdims=True)

    sqbuf[me] = sqs[...]
    rowbuf[mine] = jnp.sum(sqs[...], axis=0, keepdims=True)
    for step in range(1, ranks):
        for copy in send_sq(step):
            copy.start()

    def row_copy(i):
        peer = lax.rem(mine + i, count)
        return pltpu.make_async_remote_copy(
            src_ref=rowbuf.at[mine], dst_ref=rowbuf.at[mine], send_sem=sq_send.at[i], recv_sem=sq_recv.at[i],
            device_id=(peer // ranks, lax.rem(peer, ranks)), device_id_type=MESH,
        )

    def begin(i, c):
        row_copy(i).start()
        return c

    def finish(i, c):
        row_copy(i).wait()
        return c

    lax.fori_loop(1, count, begin, 0)
    for step in range(1, ranks):
        for copy in send_sq(step):
            copy.wait()
    group_sum = sqbuf[0]
    for z in range(1, ranks):
        group_sum = group_sum + sqbuf[z]
    norm_out[...] = jnp.transpose(jnp.sqrt(group_sum))[0:4, :]
    lax.fori_loop(1, count, finish, 0)
    everything = lax.fori_loop(0, count, lambda i, c: c + rowbuf[i], jnp.zeros((1, LANES), jnp.float32))
    tot_out[...] = jnp.sqrt(everything[:, 0:4] / (scen * groups))


def put(mis, dual, lim, norm, tot, mis_out, dual_out, lim_out, norm_out, tot_out, sems):
    copies = [pltpu.make_async_copy(mis.at[q], mis_out.at[:, q], sems.at[q]) for q in range(2)]
    rest = ((dual, dual_out), (lim, lim_out), (norm, norm_out), (tot, tot_out))
    copies += [pltpu.make_async_copy(a, b, sems.at[2 + i]) for i, (a, b) in enumerate(rest)]
    for copy in copies:
        copy.start()
    for copy in copies:
        copy.wait()


def per_device(
    base_vm, base_va, delta_state, multipliers, net_inj, ang_grad, from_bus, to_bus,
    status, conduct, suscept, charging, rating, slack, zdual,
):
    groups, ranks = lax.axis_size("ctg"), lax.axis_size("br")
    count = groups * ranks
    scen, _, nb = delta_state.shape
    nl = from_bus.shape[0]
    per = scen // ranks
    buses, rows = nb * ranks, nl // LANES
    total = rows * ranks
    pad = -(-rows // SUB) * SUB
    piece = base_vm.shape[0]
    width, group, _, entries = packing(per)
    f32, i32 = jnp.float32, jnp.int32
    vmem = pl.BlockSpec(memory_space=pltpu.VMEM)
    hbm = pl.BlockSpec(memory_space=pl.ANY)
    sem = pltpu.SemaphoreType.DMA
    kinds = 8 + 2 * per
    shapes = (
        jax.ShapeDtypeStruct((2, scen, nb), f32),
        jax.ShapeDtypeStruct((scen, nb), f32),
        jax.ShapeDtypeStruct((scen, nl), f32),
        jax.ShapeDtypeStruct((4, scen), f32),
        jax.ShapeDtypeStruct((1, 4), f32),
    )

    def lined(x):
        return x.reshape(rows, LANES)

    made = pl.pallas_call(
        functools.partial(body, groups, ranks),
        out_shape=shapes,
        in_specs=[hbm] * 16,
        out_specs=(vmem,) * 5,
        scratch_shapes=[
            pltpu.VMEM((2, 1, piece), f32),
            pltpu.VMEM((groups, 2, 1, piece), f32),
            pltpu.VMEM((2, scen, nb), f32),
            pltpu.VMEM((SUB, buses), f32),
            pltpu.VMEM((2, total, LANES), i32),
            pltpu.VMEM((3, total, LANES), f32),
            pltpu.VMEM((per, total, LANES), i32),
            pltpu.VMEM((2, total * SUB, LANES), f32),
            pltpu.VMEM((2, entries * SUB, LANES), f32),
            pltpu.VMEM((buses // SPAN * width, SPAN), f32),
            pltpu.VMEM((ranks, 3, per, nb), f32),
            pltpu.VMEM((3, scen, nb), f32),
            pltpu.VMEM((per, total, LANES), f32),
            pltpu.VMEM((scen * pad, LANES), f32),
            pltpu.VMEM((scen, LANES), f32),
            pltpu.VMEM((ranks, scen, LANES), f32),
            pltpu.VMEM((count, 1, LANES), f32),
            pltpu.VMEM((2, scen, nb), f32),
            pltpu.VMEM((scen, nb), f32),
            pltpu.VMEM((scen, nl), i32),
            pltpu.VMEM((scen, nl), f32),
            pltpu.VMEM((scen, nl), f32),
            pltpu.VMEM((rows, LANES), f32),
            sem((20 + per,)),
            sem((kinds, ranks)),
            sem((kinds, ranks)),
            sem((groups,)),
            sem((groups,)),
            sem((count,)),
            sem((count,)),
        ],
        compiler_params=pltpu.CompilerParams(
            collective_id=0, has_side_effects=True, vmem_limit_bytes=67043328
        ),
    )(
        base_vm, base_va, delta_state, multipliers, net_inj, ang_grad, lined(from_bus), lined(to_bus),
        status.reshape(scen, rows, LANES).transpose(1, 0, 2),
        lined(conduct), lined(suscept), lined(charging), lined(rating), status, slack, zdual,
    )
    mis, dual, lim, norms, tot = pl.pallas_call(
        put,
        out_shape=(jax.ShapeDtypeStruct((scen, 2, nb), f32),) + shapes[1:],
        in_specs=[vmem] * 5,
        out_specs=(hbm,) * 5,
        scratch_shapes=[sem((6,))],
    )(*made)
    return (mis, dual, lim, norms.T, tot[0])


def solution(mesh):
    placed = (
        P(("ctg", "br")), P(("ctg", "br")),
        P("ctg", None, "br"), P("ctg", None, "br"), P("ctg", None, "br"), P("ctg", "br"),
        P("br"), P("br"), P("ctg", "br"), P("br"), P("br"), P("br"), P("br"),
        P("ctg", "br"), P("ctg", "br"),
    )
    return jax.shard_map(
        per_device,
        mesh=mesh,
        in_specs=placed,
        out_specs=(P("ctg", None, "br"), P("ctg", "br"), P("ctg", "br"), P("ctg", None), P()),
        check_vma=False,
    )
```

time: 74.3 us -> 63.3 us (0.85)
  local copies, waits for them, and re-layouts: 9.08 us -> 0 us
  Pallas kernels: 64 us -> 62.5 us
    unnamed x29 -> x0, local copies, waits for them, and re-layouts: 6.77 us -> none
    another operation x7 -> x0, local copies, waits for them, and re-layouts: 1.48 us -> none  [the longest x2 0.75 us: per_device(): ends = jnp.stack([from_bus, to_bus])]
    pallas_call x1 -> x2, Pallas kernels: 64 us -> 62.5 us  [the longest x1 60.7 us: per_device(): pl.pallas_call(functools.partial(body, groups, ranks), out_shape=shapes,...]
    broadcast_in_dim x1 -> x0, local copies, waits for them, and re-layouts: 0.76 us -> none  [per_device(): rating[None, :]]
where the time goes in v1:
time: 63.3 us; the launch traced here: 63.1 us
  Pallas kernels  62.5 us (99%)
  between operations  0.65 us (1%)
    pallas_call x1, Pallas kernels, per_device(): pl.pallas_call(functools.partial(body, groups, ranks), out_shape=shapes,...  60.7 us
    pallas_call x1, Pallas kernels, per_device(): pl.pallas_call(put, out_shape=(jax.ShapeDtypeStruct((scen, 2, nb), f32),)...  1.8 us

profile of v1, /device:TPU:0, one launch (start us, length us, event | category | flops | bytes accessed | tf_op | source)
XLA Modules:
  0.0 63.1 jit_solution(8660504842293629903)
XLA Ops:
  0.6 60.7 %shard_map.182 = (f32[2,8,2560]{2,1,0:T(8,128)}, f32[8,2560]{1,0:T(8,128)}, f32[8,3328]{1,0:T(8,128)}, f32[4,8]{1,0:T(4,128)}, f32[1,4]{1,0:T(1,128)}) custom-call(f32[320]{0:T(512)} %bvm.1, f32[320]{0:T(512)} %bva.1, f32[8,2,2560]{2,1,0:T(2,128)} %delta.1, f32[8,2,2560]{2,1,0:T(2,128)} %mult.1, f32[8,2,2560]{2,1,0:T(2,128)} %net_h.1, f32[8,2560]{1,0:T(8,128)} %ang_h.1, ...), custom_call_target="tpu_custom_call" | custom-call | tf_op jit(solution)/shard_map/pallas_call | solution.py:488
  61.3 1.8 %shard_map.183 = (f32[8,2,2560]{2,1,0:T(2,128)}, f32[8,2560]{1,0:T(8,128)}, f32[8,3328]{1,0:T(8,128)}, f32[4,8]{1,0:T(4,128)}, f32[1,4]{1,0:T(1,128)}) custom-call(f32[2,8,2560]{2,1,0:T(8,128)} %get-tuple-element.15.mis, f32[8,2560]{1,0:T(8,128)} %get-tuple-element.16.dual, f32[8,3328]{1,0:T(8,128)} %get-tuple-element.17.lim, ...), custom_call_target="tpu_custom_call" | custom-call | tf_op jit(solution)/shard_map/pallas_call | solution.py:533

commit v2 on v1

--- a/solution.py
+++ b/solution.py
@@ -12,6 +12,7 @@
 SPAN = 256
 SUB = 8
 PACK = 16
+LOOP_GATHERS = 1
 MESH = pl.DeviceIdType.MESH
 
 
@@ -39,7 +40,7 @@
     groups, ranks,
     bvm, bva, delta, mult, net_h, ang_h, frm, to, status_t, con, sus, cha, rat, status_h, slack_h, zdual_h,
     mis_out, dual_out, lim_out, norm_out, tot_out,
-    bown, bslot, volts, table, ends, par, stat, picks, vals, acc, res, rbuf, flow, rflow,
+    bown, bslot, volts, table, split, ends, par, stat, picks, vals, acc, res, rbuf, flow, rflow,
     sqs, sqbuf, rowbuf, net, ang, status, slack, zdual, rate,
     local, send, recv, base_send, base_recv, sq_send, sq_recv,
 ):
@@ -185,8 +186,9 @@
         copy.wait()
     for q in range(2):
         base = jnp.concatenate([bslot[i, q] for i in range(groups)], axis=1)
-        volts[q] = volts[q] + base
-        table[q * per : (q + 1) * per, cols_of(me)] = table[q * per : (q + 1) * per, cols_of(me)] + base
+        shift = 1.0 - q
+        volts[q] = (volts[q] + base) - shift
+        table[q * per : (q + 1) * per, cols_of(me)] = (table[q * per : (q + 1) * per, cols_of(me)] + base) - shift
 
     for step in range(1, ranks):
         for copy in send_volts(step):
@@ -213,32 +215,84 @@
     def slot_of(r):
         return pl.ds(pl.multiple_of(r * SUB, SUB), SUB)
 
-    unroll = 2 if rows % 2 == 0 else 1
+    spans_here = nb // SPAN
+    half = split.shape[1] // 2
+    label = lax.broadcasted_iota(jnp.int32, (SPAN, LANES), 0).astype(bf16)
+
+    def divide(src):
+        for k in range(0, spans_here, 2):
+            wide = [
+                table[:, pl.ds(pl.multiple_of(src * nb + o * SPAN, LANES), SPAN)]
+                for o in range(k, min(k + 2, spans_here))
+            ]
+            wide = jnp.concatenate((wide * 2)[:2], axis=0)
+            head = wide.astype(bf16)
+            split[src, k * SUB : k * SUB + PACK, :] = head
+            split[src, half + k * SUB : half + k * SUB + PACK, :] = (wide - head.astype(jnp.float32)).astype(bf16)
+
+    def hot_of(end, r):
+        low = jnp.broadcast_to(ends[end, pl.ds(r, 1), :] & (SPAN - 1), (PACK, LANES)).astype(bf16)
+        low = jnp.concatenate([low] * (SPAN // PACK), axis=0)
+        return jnp.where(low == label, bf16(1), bf16(0))
+
+    def multiply(r, srcs, found):
+        hot = jnp.concatenate([hot_of(end, r) for end in range(2)], axis=1)
+        left = jnp.concatenate([split[src] for src in srcs], axis=0)
+        out = lax.dot_general(left, hot, (((1,), (0,)), ((), ())), preferred_element_type=jnp.float32)
+        for end in range(2):
+            at = slice(end * LANES, (end + 1) * LANES)
+            span = spot_of(end, r) >> 8
+            for n, src in enumerate(srcs):
+                mark = span - src * spans_here
+                for k in range(spans_here):
+                    row = 2 * n * half + k * SUB
+                    value = out[row : row + SUB, at] + out[half + row : half + row + SUB, at]
+                    found[end] = jnp.where(mark == k, value, found[end])
+        return found
+
+    def lookup(r, found, dots, gathers):
+        if dots:
+            found = multiply(r, [origin(step) for step in dots], found)
+        for step in gathers:
+            for end in range(2):
+                found[end] = look(spot_of(end, r), origin(step), found[end])
+        for end in range(2):
+            picks[end, slot_of(r), :] = found[end]
+
+    unroll = 13 if rows % 13 == 0 else 1
     early_steps = max(1, ranks // 2)
-
-    def scan_rows(src, block, fresh):
+    loop_steps = list(range(early_steps, ranks))
+    loop_gathers = loop_steps[:LOOP_GATHERS]
+    loop_dots = loop_steps[LOOP_GATHERS:]
+
+    def scan_rows(step, block):
         def some(t, c):
             for o in range(unroll):
                 r = block * rows + t * unroll + o
-                for end in range(2):
-                    start = jnp.zeros((SUB, LANES), jnp.float32) if fresh else picks[end, slot_of(r), :]
-                    picks[end, slot_of(r), :] = look(spot_of(end, r), src, start)
+                if step == 0:
+                    found = [jnp.zeros((SUB, LANES), jnp.float32)] * 2
+                else:
+                    found = [picks[end, slot_of(r), :] for end in range(2)]
+                lookup(r, found, [step], [])
             return c
 
         lax.fori_loop(0, rows // unroll, some, 0)
 
-    for block in range(ranks):
-        if block > 0:
-            for copy in send_ends(block):
+    divide(me)
+    for block in range(1, ranks):
+        for copy in send_ends(block):
+            copy.wait()
+    for step in range(early_steps):
+        if step > 0:
+            for copy in send_mult(step) + send_volts(step):
                 copy.wait()
-        scan_rows(me, origin(block), True)
-    for step in range(1, early_steps):
-        for copy in send_mult(step) + send_volts(step):
-            copy.wait()
-        lax.fori_loop(0, ranks, lambda b, c, step=step: (scan_rows(origin(step), b, False), c)[1], 0)
+            divide(origin(step))
+        lax.fori_loop(0, ranks, lambda b, c, step=step: (scan_rows(step, b), c)[1], 0)
     for step in range(early_steps, ranks):
         for copy in send_mult(step) + send_volts(step):
             copy.wait()
+    for step in loop_dots:
+        divide(origin(step))
 
     for copy in copies[middle:]:
         copy.wait()
@@ -252,22 +306,16 @@
 
     def pick(i):
         at = chunk_of(i) * SUB
-        for end in range(2):
-            for t in range(SUB):
-                r = at + t
-                spot = spot_of(end, r)
-                found = picks[end, slot_of(r), :]
-                for step in range(early_steps, ranks):
-                    found = look(spot, origin(step), found)
-                picks[end, slot_of(r), :] = found
+        for t in range(SUB):
+            r = at + t
+            lookup(r, [picks[end, slot_of(r), :] for end in range(2)], loop_dots, loop_gathers)
 
     width, group, starts, entries = packing(per)
     spans = table.shape[1] // SPAN
     tps = group // width
     parts = group // PACK
     iota16 = lax.broadcasted_iota(jnp.int32, (PACK, LANES), 0)
-    label = lax.broadcasted_iota(jnp.int32, (SPAN, LANES), 0).astype(bf16)
-    shift = [((iota16 + PACK * p) // width).astype(bf16) for p in range(parts)]
+    moved = [((iota16 + PACK * p) // width).astype(bf16) for p in range(parts)]
 
     def process(i):
         at = pl.multiple_of(chunk_of(i) * SUB, SUB)
@@ -282,7 +330,7 @@
         bh = -(b + h)
         for s in range(per):
             live = stat[s, here, :].astype(jnp.float32)
-            vf, vt = seen[0][0][s], seen[1][0][s]
+            vf, vt = 1.0 + seen[0][0][s], 1.0 + seen[1][0][s]
             sn, cs = sin_cos(seen[0][1][s] - seen[1][1][s])
             u = vf * vt
             gc_bs, gc_mbs = g * cs + b * sn, g * cs - b * sn
@@ -310,17 +358,15 @@
                 for t in (2 * pair, 2 * pair + 1):
                     spot = jnp.broadcast_to(ends[end, pl.ds(at + t, 1), :], (PACK, LANES))
                     high = (spot >> 8).astype(bf16)
-                    low = (spot & (SPAN - 1)).astype(bf16)
-                    low = jnp.concatenate([low] * (SPAN // PACK), axis=0)
-                    hots.append(jnp.where(low == label, bf16(1), bf16(0)))
-                    half = {
+                    hots.append(hot_of(end, at + t))
+                    near = {
                         s0: vals[end, pl.ds(s0 * SUB + t, SUB, stride=SUB), :] for s0 in set(starts)
                     }
                     tile = [
-                        jnp.concatenate([half[starts[2 * p]], half[starts[2 * p + 1]]], axis=0).astype(bf16)
+                        jnp.concatenate([near[starts[2 * p]], near[starts[2 * p + 1]]], axis=0).astype(bf16)
                         for p in range(parts)
                     ]
-                    level = [high - shift[p] for p in range(parts)]
+                    level = [high - moved[p] for p in range(parts)]
                     lefts.append(jnp.concatenate([
                         jnp.where(level[p] == bf16(j * tps), tile[p], bf16(0))
                         for j in range(spans // tps) for p in range(parts)
@@ -468,6 +514,7 @@
     total = rows * ranks
     pad = -(-rows // SUB) * SUB
     piece = base_vm.shape[0]
+    tall = -(-nb // SPAN // 2) * PACK
     width, group, _, entries = packing(per)
     f32, i32 = jnp.float32, jnp.int32
     vmem = pl.BlockSpec(memory_space=pltpu.VMEM)
@@ -495,6 +542,7 @@
             pltpu.VMEM((groups, 2, 1, piece), f32),
             pltpu.VMEM((2, scen, nb), f32),
             pltpu.VMEM((SUB, buses), f32),
+            pltpu.VMEM((ranks, 2 * tall, SPAN), jnp.bfloat16),
             pltpu.VMEM((2, total, LANES), i32),
             pltpu.VMEM((3, total, LANES), f32),
             pltpu.VMEM((per, total, LANES), i32),

time: 63.3 us -> 55.1 us (0.87)
  Pallas kernels: 62.5 us -> 54.3 us
    pallas_call x1, Pallas kernels: 60.7 us -> 52.5 us  [per_device(): pl.pallas_call(functools.partial(body, groups, ranks), out_shape=shapes,...]
where the time goes in v2:
time: 55.1 us; the launch traced here: 54.9 us
  Pallas kernels  54.3 us (99%)
  between operations  0.65 us (1%)
    pallas_call x1, Pallas kernels, per_device(): pl.pallas_call(functools.partial(body, groups, ranks), out_shape=shapes,...  52.5 us
    pallas_call x1, Pallas kernels, per_device(): pl.pallas_call(put, out_shape=(jax.ShapeDtypeStruct((scen, 2, nb), f32),)...  1.8 us

profile of v2, /device:TPU:0, one launch (start us, length us, event | category | flops | bytes accessed | tf_op | source)
XLA Modules:
  0.0 54.9 jit_solution(11902533591945020041)
XLA Ops:
  0.6 52.5 %shard_map.182 = (f32[2,8,2560]{2,1,0:T(8,128)}, f32[8,2560]{1,0:T(8,128)}, f32[8,3328]{1,0:T(8,128)}, f32[4,8]{1,0:T(4,128)}, f32[1,4]{1,0:T(1,128)}) custom-call(f32[320]{0:T(512)} %bvm.1, f32[320]{0:T(512)} %bva.1, f32[8,2,2560]{2,1,0:T(2,128)} %delta.1, f32[8,2,2560]{2,1,0:T(2,128)} %mult.1, f32[8,2,2560]{2,1,0:T(2,128)} %net_h.1, f32[8,2560]{1,0:T(8,128)} %ang_h.1, ...), custom_call_target="tpu_custom_call" | custom-call | tf_op jit(solution)/shard_map/pallas_call | solution.py:535
  53.1 1.8 %shard_map.183 = (f32[8,2,2560]{2,1,0:T(2,128)}, f32[8,2560]{1,0:T(8,128)}, f32[8,3328]{1,0:T(8,128)}, f32[4,8]{1,0:T(4,128)}, f32[1,4]{1,0:T(1,128)}) custom-call(f32[2,8,2560]{2,1,0:T(8,128)} %get-tuple-element.15.mis, f32[8,2560]{1,0:T(8,128)} %get-tuple-element.16.dual, f32[8,3328]{1,0:T(8,128)} %get-tuple-element.17.lim, ...), custom_call_target="tpu_custom_call" | custom-call | tf_op jit(solution)/shard_map/pallas_call | solution.py:581

commit v3 on v2

--- a/solution.py
+++ b/solution.py
@@ -12,7 +12,9 @@
 SPAN = 256
 SUB = 8
 PACK = 16
-LOOP_GATHERS = 1
+LOOP_GATHERS = 0
+LAG = 3
+LEAD = 4
 MESH = pl.DeviceIdType.MESH
 
 
@@ -39,10 +41,12 @@
 def body(
     groups, ranks,
     bvm, bva, delta, mult, net_h, ang_h, frm, to, status_t, con, sus, cha, rat, status_h, slack_h, zdual_h,
-    mis_out, dual_out, lim_out, norm_out, tot_out,
+    mis_hbm, dual_hbm, lim_hbm, norm_out, tot_out,
+    mis_out, dual_out, lim_out, out_sems,
     bown, bslot, volts, table, split, ends, par, stat, picks, vals, acc, res, rbuf, flow, rflow,
     sqs, sqbuf, rowbuf, net, ang, status, slack, zdual, rate,
     local, send, recv, base_send, base_recv, sq_send, sq_recv,
+    totals, found_at,
 ):
     grp, me = lax.axis_index("ctg"), lax.axis_index("br")
     count = groups * ranks
@@ -88,7 +92,10 @@
         return carry
 
     lax.fori_loop(1, count, greet, 0)
-    acc[...] = jnp.zeros_like(acc)
+    for q in range(2):
+        acc[...] = pltpu.matmul_pop(totals[q])
+        for slot in found_at[q]:
+            acc[0 : slot.shape[0], :] = pltpu.matmul_pop(slot)
     sqs[...] = jnp.zeros_like(sqs)
     for copy in copies[:early]:
         copy.wait()
@@ -138,10 +145,6 @@
 
     def send_sq(step):
         return [remote(sqbuf.at[me], sqbuf.at[me], 7 + 2 * per, step)]
-
-    for step in range(1, ranks):
-        for copy in send_ends(step):
-            copy.start()
 
     home = mine // groups
 
@@ -165,6 +168,11 @@
         bslot[mine - me * groups] = bown[...]
 
     for step in range(1, ranks):
+        for copy in send_ends(step):
+            copy.start()
+
+    early_steps = max(1, ranks // 2)
+    for step in range(1, early_steps + 1):
         for copy in send_mult(step):
             copy.start()
 
@@ -191,7 +199,7 @@
         table[q * per : (q + 1) * per, cols_of(me)] = (table[q * per : (q + 1) * per, cols_of(me)] + base) - shift
 
     for step in range(1, ranks):
-        for copy in send_volts(step):
+        for copy in (send_mult(step) if step > early_steps else []) + send_volts(step):
             copy.start()
     for step in range(1, ranks):
         for copy in send_par(step):
@@ -230,53 +238,65 @@
             split[src, k * SUB : k * SUB + PACK, :] = head
             split[src, half + k * SUB : half + k * SUB + PACK, :] = (wide - head.astype(jnp.float32)).astype(bf16)
 
-    def hot_of(end, r):
-        low = jnp.broadcast_to(ends[end, pl.ds(r, 1), :] & (SPAN - 1), (PACK, LANES)).astype(bf16)
-        low = jnp.concatenate([low] * (SPAN // PACK), axis=0)
-        return jnp.where(low == label, bf16(1), bf16(0))
-
-    def multiply(r, srcs, found):
-        hot = jnp.concatenate([hot_of(end, r) for end in range(2)], axis=1)
-        left = jnp.concatenate([split[src] for src in srcs], axis=0)
-        out = lax.dot_general(left, hot, (((1,), (0,)), ((), ())), preferred_element_type=jnp.float32)
+    def hot_of(r):
+        made = []
         for end in range(2):
-            at = slice(end * LANES, (end + 1) * LANES)
-            span = spot_of(end, r) >> 8
-            for n, src in enumerate(srcs):
-                mark = span - src * spans_here
+            low = jnp.broadcast_to(ends[end, pl.ds(r, 1), :] & (SPAN - 1), (PACK, LANES)).astype(bf16)
+            low = jnp.concatenate([low] * (SPAN // PACK), axis=0)
+            made.append(jnp.where(low == label, bf16(1), bf16(0)))
+        return jnp.concatenate(made, axis=1)
+
+    def multiply(r, unit, turn, steps):
+        slots = found_at[unit]
+        first = (turn * len(steps)) % (len(slots) // len(steps) * len(steps))
+        pltpu.matmul_push_rhs(hot_of(r), staging_register=0, mxu_index=unit)
+        for n, step in enumerate(steps):
+            src = origin(step)
+            pltpu.matmul_acc_lhs(slots[first + n], split[src, :half], load_staged_rhs=0 if n == 0 else None)
+            pltpu.matmul_acc_lhs(slots[first + n], split[src, half:])
+        return [slots[first + n] for n in range(len(steps))]
+
+    def choose(r, taken, steps, found):
+        for slot, step in zip(taken, steps):
+            out = pltpu.matmul_pop(slot)
+            for end in range(2):
+                at = slice(end * LANES, (end + 1) * LANES)
+                mark = (spot_of(end, r) >> 8) - origin(step) * spans_here
                 for k in range(spans_here):
-                    row = 2 * n * half + k * SUB
-                    value = out[row : row + SUB, at] + out[half + row : half + row + SUB, at]
-                    found[end] = jnp.where(mark == k, value, found[end])
-        return found
-
-    def lookup(r, found, dots, gathers):
-        if dots:
-            found = multiply(r, [origin(step) for step in dots], found)
-        for step in gathers:
+                    found[end] = jnp.where(mark == k, out[k * SUB : (k + 1) * SUB, at], found[end])
+
+    def gather(r, steps, found):
+        for step in steps:
             for end in range(2):
                 found[end] = look(spot_of(end, r), origin(step), found[end])
+
+    def keep(r, found):
         for end in range(2):
             picks[end, slot_of(r), :] = found[end]
 
-    unroll = 13 if rows % 13 == 0 else 1
-    early_steps = max(1, ranks // 2)
     loop_steps = list(range(early_steps, ranks))
     loop_gathers = loop_steps[:LOOP_GATHERS]
     loop_dots = loop_steps[LOOP_GATHERS:]
 
     def scan_rows(step, block):
-        def some(t, c):
-            for o in range(unroll):
-                r = block * rows + t * unroll + o
-                if step == 0:
-                    found = [jnp.zeros((SUB, LANES), jnp.float32)] * 2
-                else:
-                    found = [picks[end, slot_of(r), :] for end in range(2)]
-                lookup(r, found, [step], [])
-            return c
-
-        lax.fori_loop(0, rows // unroll, some, 0)
+        waiting = []
+
+        def settle():
+            r, taken = waiting.pop(0)
+            if step == 0:
+                found = [jnp.zeros((SUB, LANES), jnp.float32)] * 2
+            else:
+                found = [picks[end, slot_of(r), :] for end in range(2)]
+            choose(r, taken, [step], found)
+            keep(r, found)
+
+        for o in range(rows):
+            r = block * rows + o
+            waiting.append((r, multiply(r, o % 2, o // 2, [step])))
+            if len(waiting) > LAG:
+                settle()
+        while waiting:
+            settle()
 
     divide(me)
     for block in range(1, ranks):
@@ -304,12 +324,6 @@
     def chunk_of(i):
         return lax.rem(first + i, chunks)
 
-    def pick(i):
-        at = chunk_of(i) * SUB
-        for t in range(SUB):
-            r = at + t
-            lookup(r, [picks[end, slot_of(r), :] for end in range(2)], loop_dots, loop_gathers)
-
     width, group, starts, entries = packing(per)
     spans = table.shape[1] // SPAN
     tps = group // width
@@ -325,7 +339,6 @@
             return picks[end, pl.ds(at * SUB + q * per + s, SUB, stride=SUB), :]
 
         seen = [[[quantity(end, q, s) for s in range(per)] for q in range(4)] for end in range(2)]
-        pick(jnp.minimum(i + 1, chunks - 1))
         g, b, h = par[0, here, :], par[1, here, :], par[2, here, :]
         bh = -(b + h)
         for s in range(per):
@@ -351,34 +364,54 @@
                     for v, x in ((q * per + s, head), ((3 + q) * per + s, tail)):
                         for e in range(v, entries, width):
                             vals[end, e * SUB : (e + 1) * SUB, :] = x
-        sums = None
-        for end in range(2):
-            for pair in range(SUB // 2):
-                lefts, hots = [], []
-                for t in (2 * pair, 2 * pair + 1):
-                    spot = jnp.broadcast_to(ends[end, pl.ds(at + t, 1), :], (PACK, LANES))
-                    high = (spot >> 8).astype(bf16)
-                    hots.append(hot_of(end, at + t))
-                    near = {
-                        s0: vals[end, pl.ds(s0 * SUB + t, SUB, stride=SUB), :] for s0 in set(starts)
-                    }
-                    tile = [
-                        jnp.concatenate([near[starts[2 * p]], near[starts[2 * p + 1]]], axis=0).astype(bf16)
-                        for p in range(parts)
-                    ]
-                    level = [high - moved[p] for p in range(parts)]
-                    lefts.append(jnp.concatenate([
-                        jnp.where(level[p] == bf16(j * tps), tile[p], bf16(0))
-                        for j in range(spans // tps) for p in range(parts)
-                    ], axis=0))
-                term = lax.dot_general(
-                    jnp.concatenate(lefts, axis=1), jnp.concatenate(hots, axis=1),
-                    (((1,), (1,)), ((), ())), preferred_element_type=jnp.float32,
-                )
-                sums = term if sums is None else sums + term
-        acc[...] += sums
-
-    pick(0)
+        def left_of(t):
+            lefts = []
+            for end in range(2):
+                spot = jnp.broadcast_to(ends[end, pl.ds(at + t, 1), :], (PACK, LANES))
+                high = (spot >> 8).astype(bf16)
+                near = {s0: vals[end, pl.ds(s0 * SUB + t, SUB, stride=SUB), :] for s0 in set(starts)}
+                tile = [
+                    jnp.concatenate([near[starts[2 * p]], near[starts[2 * p + 1]]], axis=0).astype(bf16)
+                    for p in range(parts)
+                ]
+                level = [high - moved[p] for p in range(parts)]
+                lefts.append(jnp.concatenate([
+                    jnp.where(level[p] == bf16(j * tps), tile[p], bf16(0))
+                    for j in range(spans // tps) for p in range(parts)
+                ], axis=0))
+            return jnp.concatenate(lefts, axis=1)
+
+        def add(t):
+            unit = t % 2
+            pltpu.matmul_push_rhs(hot_of(at + t), staging_register=1, mxu_index=unit, transpose=True)
+            pltpu.matmul_acc_lhs(totals[unit], left_of(t), load_staged_rhs=1)
+
+        seek(i + 1, add)
+
+    def seek(i, add):
+        at = chunk_of(jnp.minimum(i, chunks - 1)) * SUB
+        waiting = []
+
+        def settle():
+            r, taken = waiting.pop(0)
+            found = [picks[end, slot_of(r), :] for end in range(2)]
+            choose(r, taken, loop_dots, found)
+            gather(r, loop_gathers, found)
+            keep(r, found)
+
+        for t in range(SUB):
+            waiting.append((at + t, multiply(at + t, t % 2, t // 2, loop_dots) if loop_dots else []))
+            if add is not None and t >= LEAD:
+                add(t - LEAD)
+            if len(waiting) > LAG:
+                settle()
+        while waiting:
+            settle()
+        if add is not None:
+            for t in range(SUB - LEAD, SUB):
+                add(t)
+
+    seek(0, None)
 
     def advance(i, c):
         done = ahead + i * SUB
@@ -400,6 +433,7 @@
 
     lax.fori_loop(0, chunks, advance, 0)
 
+    acc[...] = pltpu.matmul_pop(totals[0]) + pltpu.matmul_pop(totals[1])
     quarter = nb // SPAN
     for dest in range(ranks):
         for k in range(dest * quarter, (dest + 1) * quarter):
@@ -456,38 +490,47 @@
     dual = rbuf[2] + ang[...]
     dual_out[...] = dual
     sqs[:, 1:2] = jnp.sum(dual * dual, axis=1, keepdims=True)
+    written = [
+        pltpu.make_async_copy(a, b, out_sems.at[i])
+        for i, (a, b) in enumerate(((mis_out, mis_hbm), (dual_out, dual_hbm), (lim_out, lim_hbm)))
+    ]
+
+    def row_copy(i):
+        peer = lax.rem(mine + i, count)
+        return pltpu.make_async_remote_copy(
+            src_ref=rowbuf.at[mine], dst_ref=rowbuf.at[mine], send_sem=sq_send, recv_sem=sq_recv,
+            device_id=(peer // ranks, lax.rem(peer, ranks)), device_id_type=MESH,
+        )
+
+    def begin(i, c):
+        row_copy(i).start()
+        return c
+
+    all_rows = pltpu.make_async_remote_copy(
+        src_ref=rowbuf.at[pl.ds(0, count - 1)], dst_ref=rowbuf.at[pl.ds(0, count - 1)],
+        send_sem=sq_send, recv_sem=sq_recv, device_id=(grp, toward(1)), device_id_type=MESH,
+    )
 
     sqbuf[me] = sqs[...]
     rowbuf[mine] = jnp.sum(sqs[...], axis=0, keepdims=True)
     for step in range(1, ranks):
         for copy in send_sq(step):
             copy.start()
-
-    def row_copy(i):
-        peer = lax.rem(mine + i, count)
-        return pltpu.make_async_remote_copy(
-            src_ref=rowbuf.at[mine], dst_ref=rowbuf.at[mine], send_sem=sq_send.at[i], recv_sem=sq_recv.at[i],
-            device_id=(peer // ranks, lax.rem(peer, ranks)), device_id_type=MESH,
-        )
-
-    def begin(i, c):
-        row_copy(i).start()
-        return c
-
-    def finish(i, c):
-        row_copy(i).wait()
-        return c
-
     lax.fori_loop(1, count, begin, 0)
+    for copy in written:
+        copy.start()
     for step in range(1, ranks):
         for copy in send_sq(step):
             copy.wait()
     group_sum = sqbuf[0]
     for z in range(1, ranks):
         group_sum = group_sum + sqbuf[z]
+
     norm_out[...] = jnp.transpose(jnp.sqrt(group_sum))[0:4, :]
-    lax.fori_loop(1, count, finish, 0)
-    everything = lax.fori_loop(0, count, lambda i, c: c + rowbuf[i], jnp.zeros((1, LANES), jnp.float32))
+    for copy in written:
+        copy.wait()
+    all_rows.wait()
+    everything = jnp.sum(rowbuf[...], axis=0)
     tot_out[...] = jnp.sqrt(everything[:, 0:4] / (scen * groups))
 
 
@@ -532,12 +575,26 @@
     def lined(x):
         return x.reshape(rows, LANES)
 
+    def scoped(*refs):
+        def inner(sums, slots):
+            body(groups, ranks, *refs, sums, slots)
+
+        pl.run_scoped(
+            inner,
+            [pltpu.ACC(q)((buses // SPAN * width, SPAN), f32) for q in range(2)],
+            [[pltpu.ACC(q)((tall, SPAN), f32) for _ in range(4)] for q in range(2)],
+        )
+
     made = pl.pallas_call(
-        functools.partial(body, groups, ranks),
+        scoped,
         out_shape=shapes,
         in_specs=[hbm] * 16,
-        out_specs=(vmem,) * 5,
+        out_specs=(hbm,) * 3 + (vmem,) * 2,
         scratch_shapes=[
+            pltpu.VMEM((2, scen, nb), f32),
+            pltpu.VMEM((scen, nb), f32),
+            pltpu.VMEM((scen, nl), f32),
+            sem((3,)),
             pltpu.VMEM((2, 1, piece), f32),
             pltpu.VMEM((groups, 2, 1, piece), f32),
             pltpu.VMEM((2, scen, nb), f32),
@@ -567,8 +624,8 @@
             sem((kinds, ranks)),
             sem((groups,)),
             sem((groups,)),
-            sem((count,)),
-            sem((count,)),
+            sem,
+            sem,
         ],
         compiler_params=pltpu.CompilerParams(
             collective_id=0, has_side_effects=True, vmem_limit_bytes=67043328

time: 55.1 us -> 50.1 us (0.909)
  Pallas kernels: 54.3 us -> 49.3 us
    pallas_call x1, Pallas kernels: 52.5 us -> 47.5 us  [per_device(): pl.pallas_call(scoped, out_shape=shapes, in_specs=[hbm] * 16, out_specs=(...]
where the time goes in v3:
time: 50.1 us; the launch traced here: 49.9 us
  Pallas kernels  49.3 us (98%)
  between operations  0.65 us (1%)
    pallas_call x1, Pallas kernels, per_device(): pl.pallas_call(scoped, out_shape=shapes, in_specs=[hbm] * 16, out_specs=(...  47.5 us
    pallas_call x1, Pallas kernels, per_device(): pl.pallas_call(put, out_shape=(jax.ShapeDtypeStruct((scen, 2, nb), f32),)...  1.8 us

profile of v3, /device:TPU:0, one launch (start us, length us, event | category | flops | bytes accessed | tf_op | source)
XLA Modules:
  0.0 49.9 jit_solution(14521770426496191337)
XLA Ops:
  0.6 47.5 %shard_map.182 = (f32[2,8,2560]{2,1,0:T(8,128)}, f32[8,2560]{1,0:T(8,128)}, f32[8,3328]{1,0:T(8,128)}, f32[4,8]{1,0:T(4,128)}, f32[1,4]{1,0:T(1,128)}) custom-call(f32[320]{0:T(512)} %refs_0_.1, f32[320]{0:T(512)} %refs_1_.1, f32[8,2,2560]{2,1,0:T(2,128)} %refs_2_.1, f32[8,2,2560]{2,1,0:T(2,128)} %refs_3_.1, f32[8,2,2560]{2,1,0:T(2,128)} %refs_4_.1, ...), custom_call_target="tpu_custom_call" | custom-call | tf_op jit(solution)/shard_map/pallas_call | solution.py:588
  48.1 1.8 %shard_map.183 = (f32[8,2,2560]{2,1,0:T(2,128)}, f32[8,2560]{1,0:T(8,128)}, f32[8,3328]{1,0:T(8,128)}, f32[4,8]{1,0:T(4,128)}, f32[1,4]{1,0:T(1,128)}) custom-call(f32[2,8,2560]{2,1,0:T(8,128)} %get-tuple-element.15.mis, f32[8,2560]{1,0:T(8,128)} %get-tuple-element.16.dual, f32[8,3328]{1,0:T(8,128)} %get-tuple-element.17.lim, ...), custom_call_target="tpu_custom_call" | custom-call | tf_op jit(solution)/shard_map/pallas_call | solution.py:638

commit v4 on v3

--- a/solution.py
+++ b/solution.py
@@ -299,15 +299,19 @@
             settle()
 
     divide(me)
-    for block in range(1, ranks):
-        for copy in send_ends(block):
-            copy.wait()
     for step in range(early_steps):
         if step > 0:
             for copy in send_mult(step) + send_volts(step):
                 copy.wait()
             divide(origin(step))
-        lax.fori_loop(0, ranks, lambda b, c, step=step: (scan_rows(step, b), c)[1], 0)
+        start = 0
+        if step == 0:
+            start = 1
+            scan_rows(0, me)
+            for block in range(1, ranks):
+                for copy in send_ends(block):
+                    copy.wait()
+        lax.fori_loop(start, ranks, lambda b, c, step=step: (scan_rows(step, origin(b)), c)[1], 0)
     for step in range(early_steps, ranks):
         for copy in send_mult(step) + send_volts(step):
             copy.wait()
@@ -435,7 +439,7 @@
 
     acc[...] = pltpu.matmul_pop(totals[0]) + pltpu.matmul_pop(totals[1])
     quarter = nb // SPAN
-    for dest in range(ranks):
+    for dest in [0, *range(ranks - 1, 0, -1)]:
         for k in range(dest * quarter, (dest + 1) * quarter):
             row = (k // tps) * group + (k % tps) * width
             both = acc[row : row + 3 * per, :] + acc[row + 3 * per : row + width, :]

time: 50.1 us -> 48.8 us (0.974)
  Pallas kernels: 49.3 us -> 48 us
    pallas_call x1, Pallas kernels: 47.5 us -> 46.2 us  [per_device(): pl.pallas_call(scoped, out_shape=shapes, in_specs=[hbm] * 16, out_specs=(...]
where the time goes in v4:
time: 48.8 us; the launch traced here: 48.6 us
  Pallas kernels  48 us (98%)
  between operations  0.65 us (1%)
    pallas_call x1, Pallas kernels, per_device(): pl.pallas_call(scoped, out_shape=shapes, in_specs=[hbm] * 16, out_specs=(...  46.2 us
    pallas_call x1, Pallas kernels, per_device(): pl.pallas_call(put, out_shape=(jax.ShapeDtypeStruct((scen, 2, nb), f32),)...  1.8 us

profile of v4, /device:TPU:0, one launch (start us, length us, event | category | flops | bytes accessed | tf_op | source)
XLA Modules:
  0.0 48.6 jit_solution(9069591378204173679)
XLA Ops:
  0.6 46.2 %shard_map.182 = (f32[2,8,2560]{2,1,0:T(8,128)}, f32[8,2560]{1,0:T(8,128)}, f32[8,3328]{1,0:T(8,128)}, f32[4,8]{1,0:T(4,128)}, f32[1,4]{1,0:T(1,128)}) custom-call(f32[320]{0:T(512)} %refs_0_.1, f32[320]{0:T(512)} %refs_1_.1, f32[8,2,2560]{2,1,0:T(2,128)} %refs_2_.1, f32[8,2,2560]{2,1,0:T(2,128)} %refs_3_.1, f32[8,2,2560]{2,1,0:T(2,128)} %refs_4_.1, ...), custom_call_target="tpu_custom_call" | custom-call | tf_op jit(solution)/shard_map/pallas_call | solution.py:592
  46.8 1.8 %shard_map.183 = (f32[8,2,2560]{2,1,0:T(2,128)}, f32[8,2560]{1,0:T(8,128)}, f32[8,3328]{1,0:T(8,128)}, f32[4,8]{1,0:T(4,128)}, f32[1,4]{1,0:T(1,128)}) custom-call(f32[2,8,2560]{2,1,0:T(8,128)} %get-tuple-element.15.mis, f32[8,2560]{1,0:T(8,128)} %get-tuple-element.16.dual, f32[8,3328]{1,0:T(8,128)} %get-tuple-element.17.lim, ...), custom_call_target="tpu_custom_call" | custom-call | tf_op jit(solution)/shard_map/pallas_call | solution.py:642
